TPU v7x, 32 devices: a whole 2x2x4 slice. The times are simulated.
32 devices in a mesh: row: 2 (over core), col: 4 (over y, x), depth: 4 (over z).
Axes of the slice: x: 2, y: 2, z: 4, core: 2. Of those that a mesh axis runs over, the one named last changes fastest.
Arguments:
- a_tile: float32 [2048, 2048], P('row', 'col'), as said below
- panels: float32 [2048, 4096], P('row', 'depth'), as said below
Outputs:
- trailing: float32 [2048, 2048], P(('row', 'depth'), 'col')
- new_panel: float32 [2048, 512], P(('row', 'col'))
- diag_norm: float32 [1], replicated
Inputs may be any that keep to these rules, and one draw needn't show every extreme that they name: symmetric; a_tile - panels panels^T is positive definite with a large positive diagonal. `panels`: real-valued entries of full rank.
All inputs are finite; a program needn't handle non-finite values.
Results may differ from a plain program's by a relative error of at most 0.00015.
Values sent between devices are 32-bit elements; how exact they have to be, the bound alone decides.
A program may use at most 64 MiB of HBM per device.

v0:
```python
import jax
import jax.numpy as jnp
from jax import lax
from jax.sharding import PartitionSpec as P

PB = 512


def from_root(value, axis, source):
    kept = jnp.where(lax.axis_index(axis) == source, value, 0).astype(value.dtype)
    return lax.psum(kept, axis)


def outer_rows(left, right):
    return lax.dot_general(
        left,
        right,
        (((1,), (1,)), ((), ())),
        precision=lax.Precision.HIGHEST,
        preferred_element_type=jnp.float32,
    )


def local(a_tile, panels):
    tile_rows, tile_cols = a_tile.shape
    depth_count = lax.axis_size("depth")
    row_index = lax.axis_index("row")
    col_index = lax.axis_index("col")
    depth_index = lax.axis_index("depth")
    first = col_index * tile_cols
    every_row = lax.all_gather(panels, "row", axis=0, tiled=True)
    col_panels = lax.dynamic_slice_in_dim(every_row, first, tile_cols, 0)
    keep_base = depth_index == 0
    share_rows = tile_rows // depth_count
    trailing = lax.psum_scatter(
        jnp.where(keep_base, a_tile, 0.0) - outer_rows(panels, col_panels),
        "depth",
        scatter_dimension=0,
        tiled=True,
    )
    panel_block = lax.all_gather(trailing, "depth", axis=0, tiled=True)
    diag_block = from_root(panel_block[:PB], "row", 0)
    factor = jnp.linalg.cholesky(diag_block)
    solved = jax.scipy.linalg.solve_triangular(factor, panel_block.T, lower=True).T
    col_share = tile_rows // lax.axis_size("col")
    received = lax.all_to_all(solved, "col", split_axis=0, concat_axis=0, tiled=True)
    new_panel = received[:col_share]
    rows_global = (
        row_index * tile_rows
        + depth_index * share_rows
        + jnp.arange(share_rows, dtype=jnp.int32)[:, None]
    )
    cols_global = first + jnp.arange(tile_cols, dtype=jnp.int32)[None, :]
    squares = jnp.sum(jnp.where(rows_global == cols_global, trailing * trailing, 0.0))
    total = lax.psum(squares, ("row", "col", "depth"))
    order = tile_cols * lax.axis_size("col")
    diag_norm = jnp.sqrt(total / order).reshape(1)
    return (trailing, new_panel, diag_norm)


def solution(mesh):
    return jax.shard_map(
        local,
        mesh=mesh,
        in_specs=(P("row", "col"), P("row", "depth")),
        out_specs=(P(("row", "depth"), "col"), P(("row", "col"), None), P()),
        check_vma=False,
    )
```

profile of v0, /device:TPU:0, one launch (start us, length us, event | category | flops | bytes accessed | tf_op | source)
XLA Modules:
  0.0 379.2 jit_solution(3016540084601054819)
XLA Ops:
  7.2 0.7 all-gather.3.cloned.1.call-update
  7.9 1.9 copy.5
  9.9 22.2 %all-gather.3.cloned.1.call-done = f32[2048,1024]{1,0:T(8,128)} async-done(((f32[1024,1024]{1,0:T(8,128)}), f32[2048,1024]{1,0:T(8,128)}) %all-gather.3.cloned.1.call-update) | async-done | bytes 8388624 | tf_op jit(solution)/shard_map/all_gather | solution.py:31
  32.1 10.4 %bitcast_subtract_fusion = f32[1024,512]{0,1:T(8,128)} fusion(f32[1024,512]{0,1:T(8,128)S(1)} %copy.5, f32[1024,1024]{1,0:T(8,128)} %param.3, f32[2048,1024]{1,0:T(8,128)} %all-gather.3.cloned.1.call-done, s32[]{:T(128)S(6)} %select_n.29, pred[]{:T(512)S(6)} %eq.19), kind=kOutput, calls=%fused_computation.3 | convolution fusion | flops 6443499520 | bytes 10485765 | tf_op jit(solution)/shard_map/dot_general | solution.py:15
  42.6 44.9 %reduce-scatter.2.cloned.1.call-done = f32[256,512]{0,1:T(8,128)} async-done(((f32[1024,512]{0,1:T(8,128)}), f32[256,512]{0,1:T(8,128)}) %reduce-scatter.2.cloned.1.call-update) | async-done | bytes 524304 | tf_op jit(solution)/shard_map/reduce_scatter | solution.py:35
  87.5 0.2 all-reduce.3.cloned.1.call-start
  87.7 46.2 %all-gather.5.cloned.1.call-done = f32[1024,512]{0,1:T(8,128)} async-done(((f32[256,512]{0,1:T(8,128)}), f32[1024,512]{0,1:T(8,128)}) %all-gather.5.cloned.1.call-update) | async-done | bytes 2097168 | tf_op jit(solution)/shard_map/all_gather | solution.py:41
  133.9 2.3 slice_select_fusion
  136.3 18.4 %all-reduce.3.cloned.1.call-done = f32[512,512]{0,1:T(8,128)} async-done(((f32[512,512]{0,1:T(8,128)}), f32[512,512]{0,1:T(8,128)}) %all-reduce.3.cloned.1.call-update) | async-done | bytes 1048592 | tf_op jit(solution)/shard_map/psum | solution.py:11
  154.6 1.6 copy.6
  156.3 0.2 fusion.16
  156.6 11.7 %cholesky.103 = f32[128,128]{1,0:T(8,128)S(1)} custom-call(f32[128,128]{1,0:T(8,128)S(1)} %cholesky.263), custom_call_target="Cholesky" | custom-call | tf_op jit(solution)/shard_map/jit(cholesky)/cholesky | solution.py:43
  168.3 0.1 copy.7
  168.4 9.8 %custom-call.31 = f32[1,128,128]{1,2,0:T(8,128)S(1)} custom-call(f32[1,128,128]{2,1,0:T(8,128)S(1)} %get-tuple-element.33), custom_call_target="InvertDiagBlocksLowerTriangular" | custom-call | tf_op jit(solution)/shard_map/jit(cholesky)/cholesky | solution.py:43
  178.2 0.3 fusion.22
  178.5 0.1 copy.8
  178.7 0.3 convolution_subtract_fusion.2
  179.0 11.7 %cholesky.215 = f32[128,128]{1,0:T(8,128)S(1)} custom-call(f32[128,128]{1,0:T(8,128)S(1)} %cholesky.267), custom_call_target="Cholesky" | custom-call | tf_op jit(solution)/shard_map/jit(cholesky)/cholesky | solution.py:43
  190.7 0.1 copy.9
  190.9 10.0 %custom-call.32 = f32[1,128,128]{1,2,0:T(8,128)S(1)} custom-call(f32[1,128,128]{2,1,0:T(8,128)S(1)} %get-tuple-element.31), custom_call_target="InvertDiagBlocksLowerTriangular" | custom-call | tf_op jit(solution)/shard_map/jit(cholesky)/cholesky | solution.py:43
  200.9 0.1 cholesky.222
  201.0 0.3 convolution_dynamic-update-slice_fusion
  201.4 1.5 convolution_subtract_fusion.3
  202.9 11.7 %cholesky.236 = f32[128,128]{1,0:T(8,128)S(1)} custom-call(f32[128,128]{1,0:T(8,128)S(1)} %cholesky.272), custom_call_target="Cholesky" | custom-call | tf_op jit(solution)/shard_map/jit(cholesky)/cholesky | solution.py:43
  214.6 0.1 copy.11
  214.7 9.8 %custom-call.33 = f32[1,128,128]{1,2,0:T(8,128)S(1)} custom-call(f32[1,128,128]{2,1,0:T(8,128)S(1)} %get-tuple-element.29), custom_call_target="InvertDiagBlocksLowerTriangular" | custom-call | tf_op jit(solution)/shard_map/jit(cholesky)/cholesky | solution.py:43
  224.6 0.3 convolution_dynamic-update-slice_fusion.1
  224.9 1.3 convolution_subtract_fusion.4
  226.2 11.9 %cholesky.253 = f32[128,128]{1,0:T(8,128)S(1)} custom-call(f32[128,128]{1,0:T(8,128)S(1)} %convolution_subtract_fusion.4), custom_call_target="Cholesky" | custom-call | tf_op jit(solution)/shard_map/jit(cholesky)/cholesky | solution.py:43
  238.1 0.1 copy.13
  238.3 0.6 compare_reduce_fusion.1
  238.9 0.7 compare_reduce_fusion
  239.6 0.6 compare_reduce_fusion.2
  242.8 1.1 select_select_fusion
  243.9 12.0 %while.1 = (s32[]{:T(128)}, f32[512,512]{0,1:T(8,128)}, s32[4,2]{0,1:T(2,128)S(1)}, f32[4,128,128]{2,1,0:T(8,128)S(1)}, s32[]{:T(128)}) while((s32[]{:T(128)}, f32[512,512]{0,1:T(8,128)}, s32[4,2]{0,1:T(2,128)S(1)}, f32[4,128,128]{2,1,0:T(8,128)S(1)}, s32[]{:T(128)}) %tuple.29), condition=%wide.while_cond, body=%wide.while_body.sunk | while | flops 2 | bytes 393329 | solution.py:44
  243.9 0.1 constant_dynamic-slice_fusion.2
  244.0 0.5 fusion.47
  244.5 2.3 dynamic-slice.7
  246.8 0.1 copy.22
  246.9 0.1 constant_dynamic-slice_fusion.2
  247.0 0.5 fusion.47
  247.5 2.3 dynamic-slice.7
  249.8 0.1 copy.22
  250.0 0.5 fusion.47
  250.5 2.3 dynamic-slice.7
  252.8 0.1 copy.22
  253.0 0.5 fusion.47
  253.5 2.2 dynamic-slice.7
  255.8 0.1 copy.22
  255.9 39.3 %custom-call.34 = f32[4,128,128]{1,2,0:T(8,128)S(1)} custom-call(f32[4,128,128]{2,1,0:T(8,128)S(1)} %get-tuple-element.10), custom_call_target="InvertDiagBlocksLowerTriangular" | custom-call | tf_op jit(solution)/shard_map/jit(_solve_triangular)/triangular_solve | solution.py:44
  295.2 0.6 fusion.17
  295.9 1.5 convolution_subtract_fusion.1
  297.3 0.6 fusion.30
  298.0 1.6 convolution_subtract_fusion
  299.6 0.6 fusion.28
  300.3 2.0 fusion.10
  302.3 0.6 fusion.27
  302.9 0.1 maximum_bitcast_fusion
  303.1 1.9 copy.19
  305.0 4.1 %all-to-all-start = ((f32[4,256,512]{2,1,0:T(8,128)}), f32[4,256,512]{2,1,0:T(8,128)S(1)}, u32[]{:S(2)}, u32[]{:S(2)}) async-start(f32[4,256,512]{2,1,0:T(8,128)} %bitcast.14), calls=%async_computation.1 | async-start | bytes 4194304 | tf_op jit(solution)/shard_map/all_to_all | solution.py:46
  309.0 0.8 select_reduce_fusion
  309.9 58.8 %psum.15 = f32[]{:T(128)} all-reduce(f32[]{:T(128)} %select_reduce_fusion), channel_id=1, replica_groups=mesh['row'=2,'col'=4,'depth'=4] {'row','col','depth'}, use_global_device_ids=true, to_apply=%region_11.12 | all-reduce | flops 1 | bytes 8 | tf_op jit(solution)/shard_map/psum | solution.py:55
  369.3 1.0 copy.16
  370.3 0.8 slice_bitcast_fusion
  (37 shorter events, 0.6 us)
Async XLA Ops:
  7.2 25.0 %all-gather.3.cloned.1.call-start = ((), (), s32[]{:S(2)}) async-start(), calls=%async_computation.2 | async-start | bytes 12582912 | tf_op jit(solution)/shard_map/all_gather | solution.py:31
  7.9 79.6 %reduce-scatter.2.cloned.1.call-start = ((), (), s32[]{:S(2)}) async-start(), calls=%async_computation.3 | async-start | bytes 2621440 | tf_op jit(solution)/shard_map/reduce_scatter | solution.py:35
  42.5 91.4 %all-gather.5.cloned.1.call-start = ((), (), s32[]{:S(2)}) async-start(), calls=%async_computation.4 | async-start | bytes 2621440 | tf_op jit(solution)/shard_map/all_gather | solution.py:41
  87.5 67.1 %all-reduce.3.cloned.1.call-start = ((), (), s32[]{:S(2)}) async-start(), calls=%async_computation.5 | async-start | bytes 2097152 | tf_op jit(solution)/shard_map/psum | solution.py:11
  154.6 1.7 copy-start.2
  156.5 34.4 %copy-start.3 = (f32[512,512]{1,0:T(8,128)}, f32[512,512]{1,0:T(8,128)S(1)}, u32[]{:S(2)}) copy-start(f32[512,512]{1,0:T(8,128)S(1)} %fusion.16) | copy-start | bytes 3145732
  242.7 52.5 %copy-start = (f32[1024,512]{0,1:T(8,128)S(1)}, f32[1024,512]{0,1:T(8,128)}, u32[]{:S(2)}) copy-start(f32[1024,512]{0,1:T(8,128)} %all-gather.5.cloned.1.call-done) | copy-start | bytes 6291460
  305.0 4.1 %copy-start.1 = (f32[256,512]{0,1:T(8,128)S(1)}, f32[256,512]{0,1:T(8,128)}, u32[]{:S(2)}) copy-start(f32[256,512]{0,1:T(8,128)} %reduce-scatter.2.cloned.1.call-done) | copy-start | bytes 1572868
  305.0 65.4 %all-to-all-start = ((f32[4,256,512]{2,1,0:T(8,128)}), f32[4,256,512]{2,1,0:T(8,128)S(1)}, u32[]{:S(2)}, u32[]{:S(2)}) async-start(f32[4,256,512]{2,1,0:T(8,128)} %bitcast.14), calls=%async_computation.1 | async-start | bytes 4194304 | tf_op jit(solution)/shard_map/all_to_all | solution.py:46
Sparse Core Ops, SparseCore 0:
  9.5 22.5 all-gather.2
  42.6 44.7 reduce-scatter.1
  89.0 44.8 all-gather.4
  136.4 18.2 all-reduce.2
where the time goes:
time: 384 us; the launch traced here: 379 us
  waiting for transfers between devices  132 us (34%)
  other arithmetic  123 us (32%)
  blocking collectives  58.8 us (15%)
  matrix products  22.1 us (6%)
  local copies, waits for them, and re-layouts  19.9 us (5%)
  between operations  18.9 us (5%)
  starting transfers between devices  4.4 us (1%)
    another operation x14, other arithmetic, local(): factor = jnp.linalg.cholesky(diag_block)  78.8 us
    psum x1, blocking collectives, local(): total = lax.psum(squares, ('row', 'col', 'depth'))  58.8 us
    all_gather x1, waiting for transfers between devices, local(): panel_block = lax.all_gather(trailing, 'depth', axis=0, tiled=True)  46.2 us
    reduce_scatter x1, waiting for transfers between devices, local(): lax.psum_scatter(jnp.where(keep_base, a_tile, 0.0) - outer_rows(panels, c...  44.9 us
    another operation x3, other arithmetic, local(): jax.scipy.linalg.solve_triangular(factor, panel_block.T, lower=True)  40.4 us
    all_gather x1, waiting for transfers between devices, local(): every_row = lax.all_gather(panels, 'row', axis=0, tiled=True)  22.2 us
    psum x1, waiting for transfers between devices, from_root(): return lax.psum(kept, axis)  18.4 us
    another operation x20, local copies, waits for them, and re-layouts  11.9 us
  transfers between devices with their start and end apart: 5, of which 4 were waited for; matrix products, arithmetic and copies ran while one was open for 1% of the time, Pallas kernels for 0%

commit v1 on v0

v1 whole, which is shorter than its diff:
```python
import functools

import jax
import jax.numpy as jnp
from jax import lax
from jax.experimental import pallas as pl
from jax.experimental.pallas import tpu as pltpu
from jax.sharding import PartitionSpec as P

PB = 512
BLOCK = 128
NB = 32
CHUNK = 128
TILE = 256
HIGHEST = lax.Precision.HIGHEST
MESH = pl.DeviceIdType.MESH
F32 = jnp.float32
BF16 = jnp.bfloat16


def split(value):
    high = value.astype(BF16)
    return high, (value - high.astype(F32)).astype(BF16)


def dot_t(left, right):
    return lax.dot_general(left, right, (((1,), (1,)), ((), ())), preferred_element_type=F32)


def product(left_hi, left_lo, right_hi, right_lo):
    return dot_t(left_hi, right_hi) + (dot_t(left_hi, right_lo) + dot_t(left_lo, right_hi))


def gather_update(sizes, a_ref, p_ref, out_ref, c_ref, d_ref, n_ref, *scratch):
    nr, nc, nd = sizes
    (own_hi, own_lo, oth_hi, oth_lo, p0, pc, part, up, down, cpart, crecv, arow, nbuf, psum,
     pair_send, pair_recv, a_send, a_recv, rs_send, rs_recv, ag_send, ag_recv, d_send, d_recv,
     f_send, f_recv, up_send, up_recv, down_send, down_recv, n_send, n_recv) = scratch
    tile_rows, tile_cols = a_ref.shape
    share = tile_rows // nd
    crows = tile_rows // nc
    piece = crows // nd
    heads = PB // crows
    r, c, z = lax.axis_index("row"), lax.axis_index("col"), lax.axis_index("depth")
    chunks = tile_cols // CHUNK

    def at(row, col, depth):
        return (row, col, depth)

    def remote(src, dst, send, recv, device):
        return pltpu.make_async_remote_copy(
            src_ref=src, dst_ref=dst, send_sem=send, recv_sem=recv, device_id=device, device_id_type=MESH)

    def rows(start, size):
        return pl.ds(pl.multiple_of(start, size), size)

    barrier = pltpu.get_barrier_semaphore()
    for k in range(1, nd):
        pl.semaphore_signal(barrier, inc=1, device_id=at(r, c, lax.rem(z + k, nd)), device_id_type=MESH)
    for m in range(1, nc):
        pl.semaphore_signal(barrier, inc=1, device_id=at(r, lax.rem(c + m, nc), z), device_id_type=MESH)
    pl.semaphore_signal(barrier, inc=1, device_id=at(1 - r, c, z), device_id_type=MESH)

    @pl.loop(0, tile_rows // TILE)
    def _(t):
        hi, lo = split(p_ref[rows(t * TILE, TILE), :])
        own_hi[rows(t * TILE, TILE), :] = hi
        own_lo[rows(t * TILE, TILE), :] = lo

    pl.semaphore_wait(barrier, nd - 1 + nc - 1 + 1)

    partner = at(1 - r, c, z)
    first = c * tile_cols
    owner = first // tile_rows
    offset = lax.rem(first, tile_rows)
    head_copy = remote(p_ref.at[pl.ds(0, PB), :], p0, pair_send.at[0], pair_recv.at[0], partner)
    col_copy = remote(p_ref.at[rows(offset, tile_cols), :], pc, pair_send.at[1], pair_recv.at[1], partner)

    def a_copy(m):
        to = lax.rem(c + m, nc)
        return remote(a_ref.at[rows(to * crows + z * piece, piece), pl.ds(0, PB)], arow,
                      a_send.at[m], a_recv, at(r, to, z))

    @pl.when(r == 0)
    def _():
        head_copy.start()

    @pl.when(c == 0)
    def _():
        for m in range(1, nc):
            a_copy(m).start()

    @pl.when(r == owner)
    def _():
        col_copy.start()

    @pl.when(r == 0)
    def _():
        oth_hi[...] = own_hi[pl.ds(0, PB), :]
        oth_lo[...] = own_lo[pl.ds(0, PB), :]

    @pl.when(r != 0)
    def _():
        head_copy.wait_recv()
        hi, lo = split(p0[...])
        oth_hi[...] = hi
        oth_lo[...] = lo

    mine = rows(c * crows, crows)
    cpart[...] = product(own_hi[mine, :], own_lo[mine, :], oth_hi[...], oth_lo[...])

    def rs_copy(k):
        to = lax.rem(z + k, nd)
        return remote(cpart.at[rows(to * piece, piece), :], crecv.at[k], rs_send.at[k], rs_recv.at[k], at(r, c, to))

    for k in range(1, nd):
        rs_copy(k).start()

    @pl.when(r == owner)
    def _():
        oth_hi[...] = own_hi[rows(offset, tile_cols), :]
        oth_lo[...] = own_lo[rows(offset, tile_cols), :]

    @pl.when(r != owner)
    def _():
        col_copy.wait_recv()
        hi, lo = split(pc[...])
        oth_hi[...] = hi
        oth_lo[...] = lo

    @pl.loop(0, tile_rows // TILE)
    def _(t):
        at_rows = rows(t * TILE, TILE)
        part[at_rows, :] = product(own_hi[at_rows, :], own_lo[at_rows, :], oth_hi[...], oth_lo[...])

    @pl.when(c == 0)
    def _():
        arow[...] = a_ref[rows(z * piece, piece), pl.ds(0, PB)]

    @pl.when(c != 0)
    def _():
        a_copy(1).wait_recv()

    total = cpart[rows(z * piece, piece), :]
    for k in range(1, nd):
        rs_copy(k).wait_recv()
        total = total + crecv[k]
    c_ref[rows(z * piece, piece), :] = arow[...] - total

    def ag_copy(k):
        here = rows(z * piece, piece)
        return remote(c_ref.at[here, :], c_ref.at[here, :], ag_send.at[k], ag_recv.at[k],
                      at(r, c, lax.rem(z + k, nd)))

    def ag_from(k):
        there = rows(lax.rem(z - k + nd, nd) * piece, piece)
        return remote(c_ref.at[there, :], c_ref.at[there, :], ag_send.at[k], ag_recv.at[k], at(r, c, lax.rem(z + k, nd)))

    def d_rows(head, k):
        return rows(head * crows + lax.rem(z - k + nd, nd) * piece, piece)

    def d_copy(k, m):
        return remote(c_ref.at[rows(lax.rem(z - k + nd, nd) * piece, piece), :], d_ref.at[d_rows(c, k), :],
                      d_send.at[k, m], d_recv.at[lax.rem(c, heads), k], at(r, lax.rem(c + m, nc), z))

    def f_copy(head, k):
        return remote(d_ref.at[d_rows(head, k), :], d_ref.at[d_rows(head, k), :],
                      f_send.at[head, k], f_recv.at[head, k], partner)

    def d_from(head, k):
        return remote(d_ref.at[d_rows(head, k), :], d_ref.at[d_rows(head, k), :],
                      d_send.at[k, 0], d_recv.at[head, k], partner)

    for k in range(1, nd):
        ag_copy(k).start()
    source = jnp.logical_and(r == 0, c < heads)
    for k in range(nd):
        if k:
            ag_from(k).wait_recv()

        @pl.when(source)
        def _():
            for m in range(1, nc):
                d_copy(k, m).start()

    @pl.when(r == 0)
    def _():
        for k in range(nd):
            for head in range(heads):
                @pl.when(c == head)
                def _():
                    d_ref[d_rows(head, k), :] = c_ref[rows(lax.rem(z - k + nd, nd) * piece, piece), :]

                @pl.when(c != head)
                def _():
                    d_from(head, k).wait_recv()

                f_copy(head, k).start()

    def up_copy(b, ch):
        lanes = rows(ch * CHUNK, CHUNK)
        return remote(part.at[rows(b * share, share), lanes], up.at[rows(b * share, share), lanes],
                      up_send.at[b, ch], up_recv.at[b, ch], at(r, c, lax.rem(z + 1, nd)))

    def down_copy(b, ch):
        lanes = rows(ch * CHUNK, CHUNK)
        return remote(down_src.at[rows(b * share, share), lanes], down.at[rows(b * share, share), lanes],
                      down_send.at[b, ch], down_recv.at[b, ch], at(r, c, lax.rem(z + nd - 1, nd)))

    down_src = part

    def tick(i):
        u = i - z
        @pl.when(jnp.logical_and(u >= 0, u < (nd - z) * chunks))
        def _():
            b = nd - 1 - u // chunks
            ch = lax.rem(u, chunks)
            here = (rows(b * share, share), rows(ch * CHUNK, CHUNK))

            @pl.when(z > 0)
            def _():
                up_copy(b, ch).wait_recv()
                part[here] = part[here] + up[here]

            @pl.when(b > z)
            def _():
                up_copy(b, ch).start()

        v = i - (nd - 1 - z)
        @pl.when(jnp.logical_and(v >= 0, v < (z + 1) * chunks))
        def _():
            b = v // chunks
            ch = lax.rem(v, chunks)
            here = (rows(b * share, share), rows(ch * CHUNK, CHUNK))

            @pl.when(z < nd - 1)
            def _():
                down_copy(b, ch).wait_recv()
                part[here] = part[here] + down[here]

            @pl.when(b < z)
            def _():
                down_copy(b, ch).start()

    pl.loop(0, nd * chunks + nd - 1)(tick)

    trailing = a_ref[rows(z * share, share), :] - part[rows(z * share, share), :]
    out_ref[...] = trailing
    grow = r * tile_rows + z * share + lax.broadcasted_iota(jnp.int32, trailing.shape, 0)
    gcol = first + lax.broadcasted_iota(jnp.int32, trailing.shape, 1)
    squares = jnp.where(grow == gcol, trailing * trailing, 0.0)
    acc = squares.reshape(share // 8, 8, tile_cols).sum(0)
    acc = acc.reshape(8, chunks, CHUNK).sum(1) if chunks == 1 else sum(
        acc[:, i * CHUNK:(i + 1) * CHUNK] for i in range(chunks))
    psum[0] = acc

    stages = ((nd, lambda k: at(r, c, lax.rem(z + k, nd))), (nc, lambda k: at(r, lax.rem(c + k, nc), z)),
              (nr, lambda k: partner))
    base = 0
    for stage, (count, peer) in enumerate(stages):
        def n_copy(k):
            return remote(psum.at[stage], nbuf.at[base + k], n_send.at[base + k], n_recv.at[base + k], peer(k))
        for k in range(1, count):
            n_copy(k).start()
        for k in range(1, count):
            n_copy(k).wait_recv()
            acc = acc + nbuf[base + k]
        psum[stage + 1] = acc
        for k in range(1, count):
            n_copy(k).wait_send()
        base += count
    n_ref[...] = jnp.sqrt(jnp.sum(acc, keepdims=True) / (tile_cols * nc))

    @pl.when(r != 0)
    def _():
        for k in range(nd):
            for head in range(heads):
                f_copy(head, k).wait_recv()

    @pl.when(r == 0)
    def _():
        head_copy.wait_send()
        for k in range(nd):
            for head in range(heads):
                f_copy(head, k).wait_send()

    @pl.when(r == owner)
    def _():
        col_copy.wait_send()

    @pl.when(c == 0)
    def _():
        for m in range(1, nc):
            a_copy(m).wait_send()

    @pl.when(source)
    def _():
        for k in range(nd):
            for m in range(1, nc):
                d_copy(k, m).wait_send()

    for k in range(1, nd):
        rs_copy(k).wait_send()
        ag_copy(k).wait_send()

    @pl.loop(0, nd)
    def _(b):
        for ch in range(chunks):
            @pl.when(b > z)
            def _():
                up_copy(b, ch).wait_send()

            @pl.when(b < z)
            def _():
                down_copy(b, ch).wait_send()


def mm(a, b, dims):
    return lax.dot_general(a, b, (dims, ((), ())), precision=HIGHEST, preferred_element_type=F32)


def factor_block(block, work):
    work[:, :BLOCK] = block
    diag = lax.broadcasted_iota(jnp.int32, (BLOCK, BLOCK), 0) == lax.broadcasted_iota(jnp.int32, (BLOCK, BLOCK), 1)
    work[:, BLOCK:] = jnp.where(diag, 1.0, 0.0)
    sub = lax.broadcasted_iota(jnp.int32, (NB, BLOCK), 0)
    for j in range(0, BLOCK, NB):
        left = work[j:j + NB, :BLOCK]
        right = work[j:j + NB, BLOCK:]
        lanes = [jnp.broadcast_to(left[:, j + k:j + k + 1], (NB, BLOCK)) for k in range(NB)]
        for k in range(NB):
            inv = lax.rsqrt(lanes[k][k:k + 1])
            col = lanes[k] * inv
            for i in range(k + 1, NB):
                lanes[i] = lanes[i] - col * col[i:i + 1]
            row_l = left[k:k + 1] * inv
            row_r = right[k:k + 1] * inv
            below = jnp.where(sub > k, col, 0.0)
            left = jnp.where(sub == k, row_l, left - below * row_l)
            right = jnp.where(sub == k, row_r, right - below * row_r)
        work[j:j + NB, :BLOCK] = left
        work[j:j + NB, BLOCK:] = right
        if j + NB < BLOCK:
            both = jnp.concatenate([left, right], axis=1)
            work[j + NB:, :] = work[j + NB:, :] - mm(left[:, j + NB:], both, ((0,), (0,)))
    return work[:, BLOCK:]


def chol_solve(d_ref, c_ref, out_ref, a, c, work):
    size = d_ref.shape[0]
    a[...] = d_ref[...]
    c[...] = c_ref[...]
    for s in range(0, size, BLOCK):
        e = s + BLOCK
        inv = factor_block(a[s:e, s:e], work)
        x = mm(c[:, s:e], inv, ((1,), (1,)))
        out_ref[:, s:e] = x
        if e < size:
            u = mm(inv, a[s:e, e:], ((1,), (0,)))
            a[e:, e:] = a[e:, e:] - mm(u, u, ((0,), (0,)))
            c[:, e:] = c[:, e:] - mm(x, u, ((1,), (0,)))


def local(sizes, a_tile, panels):
    nr, nc, nd = sizes
    tile_rows, tile_cols = a_tile.shape
    k_size = panels.shape[1]
    share, crows = tile_rows // nd, tile_rows // nc
    piece, heads, chunks = crows // nd, PB // crows, tile_cols // CHUNK
    vmem = pl.BlockSpec(memory_space=pltpu.VMEM)
    shape = lambda *s: jax.ShapeDtypeStruct(s, F32)
    dma = lambda *s: pltpu.SemaphoreType.DMA(s)
    wide = max(PB, tile_cols)
    trailing, rows_c, diag, norm = pl.pallas_call(
        functools.partial(gather_update, sizes),
        out_shape=(shape(share, tile_cols), shape(crows, PB), shape(PB, PB), shape(1, 1)),
        in_specs=[vmem] * 2,
        out_specs=(vmem,) * 4,
        scratch_shapes=[
            pltpu.VMEM((tile_rows, k_size), BF16), pltpu.VMEM((tile_rows, k_size), BF16),
            pltpu.VMEM((wide, k_size), BF16), pltpu.VMEM((wide, k_size), BF16),
            pltpu.VMEM((PB, k_size), F32), pltpu.VMEM((tile_cols, k_size), F32),
            pltpu.VMEM((tile_rows, tile_cols), F32), pltpu.VMEM((tile_rows, tile_cols), F32),
            pltpu.VMEM((tile_rows, tile_cols), F32), pltpu.VMEM((crows, PB), F32),
            pltpu.VMEM((nd, piece, PB), F32), pltpu.VMEM((piece, PB), F32),
            pltpu.VMEM((nr + nc + nd, 8, CHUNK), F32), pltpu.VMEM((4, 8, CHUNK), F32),
            dma(2), dma(2), dma(nc), pltpu.SemaphoreType.DMA, dma(nd), dma(nd), dma(nd), dma(nd),
            dma(nd, nc), dma(heads, nd), dma(heads, nd), dma(heads, nd),
            dma(nd, chunks), dma(nd, chunks), dma(nd, chunks), dma(nd, chunks),
            dma(nr + nc + nd), dma(nr + nc + nd),
        ],
        compiler_params=pltpu.CompilerParams(collective_id=0, has_side_effects=True, vmem_limit_bytes=60 << 20),
        name="gather_update",
    )(a_tile, panels)
    new_panel = pl.pallas_call(
        chol_solve,
        out_shape=shape(crows, PB),
        in_specs=[vmem] * 2,
        out_specs=vmem,
        scratch_shapes=[pltpu.VMEM((PB, PB), F32), pltpu.VMEM((crows, PB), F32), pltpu.VMEM((BLOCK, 2 * BLOCK), F32)],
        name="chol_solve",
    )(diag, rows_c)
    return (trailing, new_panel, norm.reshape(1))


def solution(mesh):
    sizes = tuple(mesh.shape[axis] for axis in ("row", "col", "depth"))
    return jax.shard_map(
        functools.partial(local, sizes),
        mesh=mesh,
        in_specs=(P("row", "col"), P("row", "depth")),
        out_specs=(P(("row", "depth"), "col"), P(("row", "col"), None), P()),
        check_vma=False,
    )
```

time: 384 us -> 111 us (0.29); the launches traced: 379 us -> 111 us
  waiting for transfers between devices: 132 us -> 0 us
  other arithmetic: 123 us -> 0 us
  Pallas kernels: 0 us -> 107 us
  blocking collectives: 58.8 us -> 0 us
  matrix products: 22.1 us -> 0 us
  local copies, waits for them, and re-layouts: 19.9 us -> 1.87 us
  between operations: 18.9 us -> 2.38 us
  starting transfers between devices: 4.4 us -> 0 us
    another operation x17 -> x0, other arithmetic: 119 us -> none  [the longest x14 78.8 us: local(): factor = jnp.linalg.cholesky(diag_block)]
    pallas_call x0 -> x2, Pallas kernels: none -> 107 us  [the longest x1 88.6 us: local(): pl.pallas_call(functools.partial(gather_update, sizes), out_shape=(shape(...]
    all_gather x2 -> x0, waiting for transfers between devices: 68.4 us -> none  [the longest x1 46.2 us: local(): panel_block = lax.all_gather(trailing, 'depth', axis=0, tiled=True)]
    psum x1 -> x0, blocking collectives: 58.8 us -> none  [local(): total = lax.psum(squares, ('row', 'col', 'depth'))]
    reduce_scatter x1 -> x0, waiting for transfers between devices: 44.9 us -> none  [local(): lax.psum_scatter(jnp.where(keep_base, a_tile, 0.0) - outer_rows(panels, c...]
    psum x1 -> x0, waiting for transfers between devices: 18.4 us -> none  [from_root(): return lax.psum(kept, axis)]
    another operation x34 -> x0, local copies, waits for them, and re-layouts: 12.6 us -> none
    another operation x13 -> x0, matrix products: 11.7 us -> none  [the longest x7 7.64 us: local(): jax.scipy.linalg.solve_triangular(factor, panel_block.T, lower=True)]
  transfers between devices with their start and end apart: 5 -> 0, of which waited for: 4 -> 0; matrix products, arithmetic and copies ran while one was open for 1% -> 0% of each run, Pallas kernels for 0% -> 0%
where the time goes in v1:
time: 111 us
  Pallas kernels  107 us (96%)
  between operations  2.38 us (2%)
  local copies, waits for them, and re-layouts  1.87 us (2%)
    pallas_call x1, Pallas kernels, local(): pl.pallas_call(functools.partial(gather_update, sizes), out_shape=(shape(...  88.6 us
    pallas_call x1, Pallas kernels, local(): pl.pallas_call(chol_solve, out_shape=shape(crows, PB), in_specs=[vmem] *...  18.4 us

profile of v1, /device:TPU:0, one launch (start us, length us, event | category | flops | bytes accessed | tf_op | source)
XLA Modules:
  0.0 111.2 jit_solution(17882610289439735313)
XLA Ops:
  0.6 88.6 %gather_update.1 = (f32[256,512]{1,0:T(8,128)}, f32[256,512]{1,0:T(8,128)}, f32[512,512]{1,0:T(8,128)}, f32[1,1]{1,0:T(1,128)}) custom-call(f32[1024,512]{1,0:T(8,128)} %a_ref.1, f32[1024,1024]{1,0:T(8,128)} %p_ref.1), custom_call_target="tpu_custom_call" | custom-call | tf_op jit(solution)/shard_map/gather_update/pallas_call | solution.py:374
  89.3 18.4 %chol_solve.1 = f32[256,512]{1,0:T(8,128)} custom-call(f32[512,512]{1,0:T(8,128)} %get-tuple-element.8.d_ref, f32[256,512]{1,0:T(8,128)} %get-tuple-element.9.c_ref), custom_call_target="tpu_custom_call" | custom-call | tf_op jit(solution)/shard_map/chol_solve/pallas_call | solution.py:395
  107.6 1.9 %copy.7 = f32[256,512]{1,0:T(8,128)} copy(f32[256,512]{1,0:T(8,128)} %get-tuple-element.14) | data formatting | bytes 1048576

commit v2 on v1

v2 whole, which is shorter than its diff:
```python
import functools

import jax
import jax.numpy as jnp
from jax import lax
from jax.experimental import pallas as pl
from jax.experimental.pallas import tpu as pltpu
from jax.sharding import PartitionSpec as P

PB = 512
BLOCK = 128
NB = 32
CHUNK = 128
EARLY = 3
TILE = 256
HIGHEST = lax.Precision.HIGHEST
MESH = pl.DeviceIdType.MESH
F32 = jnp.float32
BF16 = jnp.bfloat16


def split(value):
    high = value.astype(BF16)
    return high, (value - high.astype(F32)).astype(BF16)


def dot_t(left, right):
    return lax.dot_general(left, right, (((1,), (1,)), ((), ())), preferred_element_type=F32)


def product(left_hi, left_lo, right_hi, right_lo):
    return dot_t(left_hi, right_hi) + (dot_t(left_hi, right_lo) + dot_t(left_lo, right_hi))


def mm(a, b, dims):
    return lax.dot_general(a, b, (dims, ((), ())), precision=HIGHEST, preferred_element_type=F32)


def factor_block(work, block, advance):
    work[:, :BLOCK] = block
    diag = lax.broadcasted_iota(jnp.int32, (BLOCK, BLOCK), 0) == lax.broadcasted_iota(jnp.int32, (BLOCK, BLOCK), 1)
    work[:, BLOCK:] = jnp.where(diag, 1.0, 0.0)
    sub = lax.broadcasted_iota(jnp.int32, (NB, BLOCK), 0)
    for j in range(0, BLOCK, NB):
        left = work[j:j + NB, :BLOCK]
        right = work[j:j + NB, BLOCK:]
        advance()
        lanes = [jnp.broadcast_to(left[:, j + k:j + k + 1], (NB, BLOCK)) for k in range(NB)]
        for k in range(NB):
            inv = lax.rsqrt(lanes[k][k:k + 1])
            col = lanes[k] * inv
            for i in range(k + 1, NB):
                lanes[i] = lanes[i] - col * col[i:i + 1]
            row_l = left[k:k + 1] * inv
            row_r = right[k:k + 1] * inv
            below = jnp.where(sub > k, col, 0.0)
            left = jnp.where(sub == k, row_l, left - below * row_l)
            right = jnp.where(sub == k, row_r, right - below * row_r)
        work[j:j + NB, :BLOCK] = left
        work[j:j + NB, BLOCK:] = right
        if j + NB < BLOCK:
            both = jnp.concatenate([left, right], axis=1)
            work[j + NB:, :] = work[j + NB:, :] - mm(left[:, j + NB:], both, ((0,), (0,)))
    return work[:, BLOCK:]


def gather_update(sizes, split_d, a_ref, p_ref, out_ref, x_ref, n_ref, *scratch):
    nr, nc, nd = sizes
    (own_hi, own_lo, oth_hi, oth_lo, p0, pc, part, up, down, cpart, crecv, arow, nbuf, psum,
     pair_send, pair_recv, a_send, a_recv, rs_send, rs_recv, ag_send, ag_recv, d_send, d_recv,
     f_send, f_recv, up_send, up_recv, down_send, down_recv, n_send, n_recv,
     c_ref, d_ref, work, invs, fact, rest, dpart, drecv, adiag, ds_send, ds_recv, da_send, da_recv, ad_send, ad_recv) = scratch
    tile_rows, tile_cols = a_ref.shape
    share = tile_rows // nd
    crows = tile_rows // nc
    piece = crows // nd
    slab = PB // nc
    d_high, d_wide = split_d
    r, c, z = lax.axis_index("row"), lax.axis_index("col"), lax.axis_index("depth")
    chunks = tile_cols // CHUNK

    def at(row, col, depth):
        return (row, col, depth)

    def remote(src, dst, send, recv, device):
        return pltpu.make_async_remote_copy(
            src_ref=src, dst_ref=dst, send_sem=send, recv_sem=recv, device_id=device, device_id_type=MESH)

    def rows(start, size):
        return pl.ds(pl.multiple_of(start, size), size)

    barrier = pltpu.get_barrier_semaphore()
    for k in range(1, nd):
        pl.semaphore_signal(barrier, inc=1, device_id=at(r, c, lax.rem(z + k, nd)), device_id_type=MESH)
    for m in range(1, nc):
        pl.semaphore_signal(barrier, inc=1, device_id=at(r, lax.rem(c + m, nc), z), device_id_type=MESH)
    pl.semaphore_signal(barrier, inc=1, device_id=at(1 - r, c, z), device_id_type=MESH)

    def split_own(t):
        hi, lo = split(p_ref[rows(t * TILE, TILE), :])
        own_hi[rows(t * TILE, TILE), :] = hi
        own_lo[rows(t * TILE, TILE), :] = lo

    pl.loop(0, PB // TILE)(split_own)
    pl.semaphore_wait(barrier, nd - 1 + nc - 1 + 1)

    partner = at(1 - r, c, z)
    first = c * tile_cols
    owner = first // tile_rows
    offset = lax.rem(first, tile_rows)
    head_copy = remote(p_ref.at[pl.ds(0, PB), :], p0, pair_send.at[0], pair_recv.at[0], partner)
    col_copy = remote(p_ref.at[rows(offset, tile_cols), :], pc, pair_send.at[1], pair_recv.at[1], partner)

    def a_copy(m):
        to = lax.rem(c + m, nc)
        return remote(a_ref.at[rows(to * crows + z * piece, piece), pl.ds(0, PB)], arow,
                      a_send.at[m], a_recv, at(r, to, z))

    def patch(depth):
        return (rows(depth // (PB // d_wide) * d_high, d_high),
                rows(lax.rem(depth, PB // d_wide) * d_wide, d_wide))

    def in_slab(col, depth):
        high, wide = patch(depth)
        return (rows(col * slab + depth // (PB // d_wide) * d_high, d_high), wide)

    def ad_copy(m):
        to = lax.rem(c + m, nc)
        return remote(a_ref.at[in_slab(to, z)], adiag, ad_send.at[m], ad_recv, at(r, to, z))

    def ds_copy(k):
        to = lax.rem(z + k, nd)
        return remote(dpart.at[patch(to)], drecv.at[k], ds_send.at[k], ds_recv.at[k], at(r, c, to))

    def da_copy(k):
        here = d_ref.at[in_slab(c, z)]
        return remote(here, here, da_send.at[k], da_recv.at[k], at(r, c, lax.rem(z + k, nd)))

    def da_from(k):
        there = d_ref.at[in_slab(c, lax.rem(z - k + nd, nd))]
        return remote(there, there, da_send.at[k], da_recv.at[k], at(r, c, lax.rem(z + k, nd)))

    @pl.when(r == 0)
    def _():
        head_copy.start()

        @pl.when(c == 0)
        def _():
            for m in range(1, nc):
                ad_copy(m).start()

    @pl.when(c == 0)
    def _():
        for m in range(1, nc):
            a_copy(m).start()

    @pl.when(r == owner)
    def _():
        col_copy.start()

    @pl.when(r == 0)
    def _():
        oth_hi[...] = own_hi[pl.ds(0, PB), :]
        oth_lo[...] = own_lo[pl.ds(0, PB), :]
        band = rows(c * slab, slab)
        dpart[...] = product(own_hi[band, :], own_lo[band, :], oth_hi[...], oth_lo[...])
        for k in range(1, nd):
            ds_copy(k).start()

    pl.loop(PB // TILE, tile_rows // TILE)(split_own)

    @pl.when(r != 0)
    def _():
        head_copy.wait_recv()
        hi, lo = split(p0[...])
        oth_hi[...] = hi
        oth_lo[...] = lo

    mine = rows(c * crows, crows)
    cpart[...] = product(own_hi[mine, :], own_lo[mine, :], oth_hi[...], oth_lo[...])

    def rs_copy(k):
        to = lax.rem(z + k, nd)
        return remote(cpart.at[rows(to * piece, piece), :], crecv.at[k], rs_send.at[k], rs_recv.at[k], at(r, c, to))

    for k in range(1, nd):
        rs_copy(k).start()

    @pl.when(r == 0)
    def _():
        @pl.when(c == 0)
        def _():
            adiag[...] = a_ref[in_slab(0, z)]

        @pl.when(c != 0)
        def _():
            ad_copy(1).wait_recv()

        dsum = dpart[patch(z)]
        for k in range(1, nd):
            ds_copy(k).wait_recv()
            dsum = dsum + drecv[k]
        d_ref[in_slab(c, z)] = adiag[...] - dsum
        for k in range(1, nd):
            da_copy(k).start()

    @pl.when(r == owner)
    def _():
        oth_hi[...] = own_hi[rows(offset, tile_cols), :]
        oth_lo[...] = own_lo[rows(offset, tile_cols), :]

    @pl.when(r != owner)
    def _():
        col_copy.wait_recv()
        hi, lo = split(pc[...])
        oth_hi[...] = hi
        oth_lo[...] = lo

    @pl.loop(0, tile_rows // TILE)
    def _(t):
        at_rows = rows(t * TILE, TILE)
        part[at_rows, :] = product(own_hi[at_rows, :], own_lo[at_rows, :], oth_hi[...], oth_lo[...])

    def d_piece(col, k):
        return d_ref.at[in_slab(col, lax.rem(z - k + nd, nd))]

    def d_copy(k, m):
        return remote(d_piece(c, k), d_piece(c, k), d_send.at[k, m], d_recv.at[k, m], at(r, lax.rem(c + m, nc), z))

    def d_from(k, m):
        there = d_piece(lax.rem(c - m + nc, nc), k)
        return remote(there, there, d_send.at[k, m], d_recv.at[k, m], at(r, lax.rem(c + m, nc), z))

    def f_copy(k, m):
        there = d_piece(lax.rem(c - m + nc, nc), k)
        return remote(there, there, f_send.at[k, m], f_recv.at[k, m], partner)

    @pl.when(r == 0)
    def _():
        for k in range(nd):
            if k:
                da_from(k).wait_recv()
            for m in range(1, nc):
                d_copy(k, m).start()
            f_copy(k, 0).start()

    @pl.when(c == 0)
    def _():
        arow[...] = a_ref[rows(z * piece, piece), pl.ds(0, PB)]

    @pl.when(c != 0)
    def _():
        a_copy(1).wait_recv()

    total = cpart[rows(z * piece, piece), :]
    for k in range(1, nd):
        rs_copy(k).wait_recv()
        total = total + crecv[k]
    c_ref[rows(z * piece, piece), :] = arow[...] - total

    def ag_copy(k):
        here = rows(z * piece, piece)
        return remote(c_ref.at[here, :], c_ref.at[here, :], ag_send.at[k], ag_recv.at[k],
                      at(r, c, lax.rem(z + k, nd)))

    def ag_from(k):
        there = rows(lax.rem(z - k + nd, nd) * piece, piece)
        return remote(c_ref.at[there, :], c_ref.at[there, :], ag_send.at[k], ag_recv.at[k], at(r, c, lax.rem(z + k, nd)))

    for k in range(1, nd):
        ag_copy(k).start()

    def up_copy(b, ch):
        lanes = rows(ch * CHUNK, CHUNK)
        return remote(part.at[rows(b * share, share), lanes], up.at[rows(b * share, share), lanes],
                      up_send.at[b, ch], up_recv.at[b, ch], at(r, c, lax.rem(z + 1, nd)))

    def down_copy(b, ch):
        lanes = rows(ch * CHUNK, CHUNK)
        return remote(part.at[rows(b * share, share), lanes], down.at[rows(b * share, share), lanes],
                      down_send.at[b, ch], down_recv.at[b, ch], at(r, c, lax.rem(z + nd - 1, nd)))

    def tick(i):
        u = i - z
        @pl.when(jnp.logical_and(u >= 0, u < (nd - z) * chunks))
        def _():
            b = nd - 1 - u // chunks
            ch = lax.rem(u, chunks)
            here = (rows(b * share, share), rows(ch * CHUNK, CHUNK))

            @pl.when(z > 0)
            def _():
                up_copy(b, ch).wait_recv()
                part[here] = part[here] + up[here]

            @pl.when(b > z)
            def _():
                up_copy(b, ch).start()

        v = i - (nd - 1 - z)
        @pl.when(jnp.logical_and(v >= 0, v < (z + 1) * chunks))
        def _():
            b = v // chunks
            ch = lax.rem(v, chunks)
            here = (rows(b * share, share), rows(ch * CHUNK, CHUNK))

            @pl.when(z < nd - 1)
            def _():
                down_copy(b, ch).wait_recv()
                part[here] = part[here] + down[here]

            @pl.when(b < z)
            def _():
                down_copy(b, ch).start()

    ticks = nd * chunks + nd - 1
    slots = PB // NB + EARLY
    done = []

    def advance(last=False):
        first_tick = len(done) * ticks // slots
        done.append(None)
        pl.loop(first_tick, ticks if last else min(ticks, len(done) * ticks // slots))(tick)

    for _ in range(EARLY):
        advance()

    @pl.when(r == 0)
    def _():
        for k in range(nd):
            for m in range(1, nc):
                d_from(k, m).wait_recv()
                f_copy(k, m).start()

    @pl.when(r != 0)
    def _():
        for k in range(nd):
            for m in range(nc):
                f_copy(k, m).wait_recv()

    for s in range(0, PB, BLOCK):
        e = s + BLOCK
        inv = factor_block(work, (fact if s else d_ref)[s:e, s:e], advance)
        invs[s // BLOCK] = inv
        if e < PB:
            u = mm(inv, (fact if s else d_ref)[s:e, e:], ((1,), (0,)))
            fact[s:e, e:] = u
            fact[e:, e:] = (fact if s else d_ref)[e:, e:] - mm(u, u, ((0,), (0,)))

    for k in range(1, nd):
        ag_from(k).wait_recv()
    rest[...] = c_ref[...]
    for s in range(0, PB, BLOCK):
        e = s + BLOCK
        x = mm(rest[:, s:e], invs[s // BLOCK], ((1,), (1,)))
        x_ref[:, s:e] = x
        if e < PB:
            rest[:, e:] = rest[:, e:] - mm(x, fact[s:e, e:], ((1,), (0,)))

    trailing = a_ref[rows(z * share, share), :] - part[rows(z * share, share), :]
    out_ref[...] = trailing
    grow = r * tile_rows + z * share + lax.broadcasted_iota(jnp.int32, trailing.shape, 0)
    gcol = first + lax.broadcasted_iota(jnp.int32, trailing.shape, 1)
    squares = jnp.where(grow == gcol, trailing * trailing, 0.0)
    acc = squares.reshape(share // 8, 8, tile_cols).sum(0)
    acc = acc.reshape(8, chunks, CHUNK).sum(1) if chunks == 1 else sum(
        acc[:, i * CHUNK:(i + 1) * CHUNK] for i in range(chunks))
    psum[0] = acc

    stages = ((nd, lambda k: at(r, c, lax.rem(z + k, nd))), (nc, lambda k: at(r, lax.rem(c + k, nc), z)),
              (nr, lambda k: partner))
    base = 0
    for stage, (count, peer) in enumerate(stages):
        def n_copy(k):
            return remote(psum.at[stage], nbuf.at[base + k], n_send.at[base + k], n_recv.at[base + k], peer(k))
        for k in range(1, count):
            n_copy(k).start()
        for k in range(1, count):
            n_copy(k).wait_recv()
            acc = acc + nbuf[base + k]
        psum[stage + 1] = acc
        for k in range(1, count):
            n_copy(k).wait_send()
        base += count
    n_ref[...] = jnp.sqrt(jnp.sum(acc, keepdims=True) / (tile_cols * nc))

    @pl.when(r == 0)
    def _():
        head_copy.wait_send()

        @pl.when(c == 0)
        def _():
            for m in range(1, nc):
                ad_copy(m).wait_send()

        for k in range(nd):
            for m in range(nc):
                f_copy(k, m).wait_send()
                if m:
                    d_copy(k, m).wait_send()
            if k:
                ds_copy(k).wait_send()
                da_copy(k).wait_send()

    @pl.when(r == owner)
    def _():
        col_copy.wait_send()

    @pl.when(c == 0)
    def _():
        for m in range(1, nc):
            a_copy(m).wait_send()

    for k in range(1, nd):
        rs_copy(k).wait_send()
        ag_copy(k).wait_send()

    @pl.loop(0, nd)
    def _(b):
        for ch in range(chunks):
            @pl.when(b > z)
            def _():
                up_copy(b, ch).wait_send()

            @pl.when(b < z)
            def _():
                down_copy(b, ch).wait_send()


def local(sizes, a_tile, panels):
    nr, nc, nd = sizes
    tile_rows, tile_cols = a_tile.shape
    k_size = panels.shape[1]
    share, crows = tile_rows // nd, tile_rows // nc
    piece, chunks, slab = crows // nd, tile_cols // CHUNK, PB // nc
    high = max(8, slab // nd)
    split_d = (high, slab * PB // (nd * high))
    vmem = pl.BlockSpec(memory_space=pltpu.VMEM)
    shape = lambda *s: jax.ShapeDtypeStruct(s, F32)
    dma = lambda *s: pltpu.SemaphoreType.DMA(s)
    wide = max(PB, tile_cols)
    trailing, new_panel, norm = pl.pallas_call(
        functools.partial(gather_update, sizes, split_d),
        out_shape=(shape(share, tile_cols), shape(crows, PB), shape(1, 1)),
        in_specs=[vmem] * 2,
        out_specs=(vmem,) * 3,
        scratch_shapes=[
            pltpu.VMEM((tile_rows, k_size), BF16), pltpu.VMEM((tile_rows, k_size), BF16),
            pltpu.VMEM((wide, k_size), BF16), pltpu.VMEM((wide, k_size), BF16),
            pltpu.VMEM((PB, k_size), F32), pltpu.VMEM((tile_cols, k_size), F32),
            pltpu.VMEM((tile_rows, tile_cols), F32), pltpu.VMEM((tile_rows, tile_cols), F32),
            pltpu.VMEM((tile_rows, tile_cols), F32), pltpu.VMEM((crows, PB), F32),
            pltpu.VMEM((nd, piece, PB), F32), pltpu.VMEM((piece, PB), F32),
            pltpu.VMEM((nr + nc + nd, 8, CHUNK), F32), pltpu.VMEM((4, 8, CHUNK), F32),
            dma(2), dma(2), dma(nc), pltpu.SemaphoreType.DMA, dma(nd), dma(nd), dma(nd), dma(nd),
            dma(nd, nc), dma(nd, nc), dma(nd, nc), dma(nd, nc),
            dma(nd, chunks), dma(nd, chunks), dma(nd, chunks), dma(nd, chunks),
            dma(nr + nc + nd), dma(nr + nc + nd),
            pltpu.VMEM((crows, PB), F32), pltpu.VMEM((PB, PB), F32), pltpu.VMEM((BLOCK, 2 * BLOCK), F32),
            pltpu.VMEM((PB // BLOCK, BLOCK, BLOCK), F32), pltpu.VMEM((PB, PB), F32), pltpu.VMEM((crows, PB), F32),
            pltpu.VMEM((slab, PB), F32), pltpu.VMEM((nd, *split_d), F32), pltpu.VMEM(split_d, F32),
            dma(nd), dma(nd), dma(nd), dma(nd), dma(nc), pltpu.SemaphoreType.DMA,
        ],
        compiler_params=pltpu.CompilerParams(collective_id=0, has_side_effects=True, vmem_limit_bytes=60 << 20),
        name="gather_update",
    )(a_tile, panels)
    return (trailing, new_panel, norm.reshape(1))


def solution(mesh):
    sizes = tuple(mesh.shape[axis] for axis in ("row", "col", "depth"))
    return jax.shard_map(
        functools.partial(local, sizes),
        mesh=mesh,
        in_specs=(P("row", "col"), P("row", "depth")),
        out_specs=(P(("row", "depth"), "col"), P(("row", "col"), None), P()),
        check_vma=False,
    )
```

time: 111 us -> 107 us (0.964)
  Pallas kernels: 107 us -> 101 us
  local copies, waits for them, and re-layouts: 1.87 us -> 3.74 us
    pallas_call x2 -> x1, Pallas kernels: 107 us -> 101 us  [local(): pl.pallas_call(functools.partial(gather_update, sizes, split_d), out_shap...]
    unnamed x1 -> x2, local copies, waits for them, and re-layouts: 1.87 us -> 3.74 us
where the time goes in v2:
time: 107 us
  Pallas kernels  101 us (94%)
  local copies, waits for them, and re-layouts  3.74 us (3%)
  between operations  2.33 us (2%)
    pallas_call x1, Pallas kernels, local(): pl.pallas_call(functools.partial(gather_update, sizes, split_d), out_shap...  101 us
    unnamed x2, local copies, waits for them, and re-layouts  3.74 us

profile of v2, /device:TPU:0, one launch (start us, length us, event | category | flops | bytes accessed | tf_op | source)
XLA Modules:
  0.0 107.1 jit_solution(18383677319006580729)
XLA Ops:
  0.6 101.0 %gather_update.1 = (f32[256,512]{1,0:T(8,128)}, f32[256,512]{1,0:T(8,128)}, f32[1,1]{1,0:T(1,128)}) custom-call(f32[1024,512]{1,0:T(8,128)} %a_ref.1, f32[1024,1024]{1,0:T(8,128)} %p_ref.1), custom_call_target="tpu_custom_call" | custom-call | tf_op jit(solution)/shard_map/gather_update/pallas_call | solution.py:442
  101.7 1.9 %copy.8 = f32[256,512]{1,0:T(8,128)} copy(f32[256,512]{1,0:T(8,128)} %get-tuple-element.12) | data formatting | bytes 1048576
  103.5 1.9 %copy.9 = f32[256,512]{1,0:T(8,128)} copy(f32[256,512]{1,0:T(8,128)} %get-tuple-element.13) | data formatting | bytes 1048576
